TPU v7x, 128 devices: a whole 4x4x4 slice. The times are simulated.
128 devices in a mesh: ctx: 16 (over x, y), head: 8 (over z, core).
Axes of the slice: x: 4, y: 4, z: 4, core: 2. Of those that a mesh axis runs over, the one named last changes fastest.
Arguments:
- query_low: bfloat16 [2, 1536], P(None, 'ctx'), may hold values from -6 to 6
- query_weight: bfloat16 [1536, 73728], P('ctx', 'head'), may hold values from -0.21875 to 0.21875
- latent_cache: bfloat16 [2, 131072, 576], P(None, ('ctx', 'head')), may hold values from -300 to 300
- lengths: int32 [2], replicated, may hold values from 81921 to 131072
- value_weight: bfloat16 [128, 512, 128], P('head'), may hold values from -2 to 2
- output_weight: bfloat16 [16384, 7168], P('head', 'ctx'), may hold values from -0.0625 to 0.0625
Outputs:
- attended: bfloat16 [2, 7168], P(None, ('ctx', 'head'))
All inputs are finite; a program needn't handle non-finite values.
Results may differ from a plain program's by a relative error of at most 0.028.
Values may be sent and summed in bfloat16 or wider, within the bound.
No kernel may reach another device: no remote copies, remote signals or barrier semaphores. Data moves between devices by JAX's collectives and lax.ppermute only.
A program may use at most 192 MiB of HBM per device.

v0:
```python
import jax
import jax.numpy as jnp
from jax import lax
from jax.sharding import Mesh
from jax.sharding import PartitionSpec as P

KV_RANK = 512
CTX = ("ctx_0", "ctx_1")
HEAD = ("head_0", "head_1")
CTX_HEAD = ("ctx_0", "ctx_1", "head_0", "head_1")
softmax_scale = 0.07216878


def sent_to_all(x, axis):
    copies = jnp.broadcast_to(x, (lax.axis_size(axis), *x.shape))
    return lax.all_to_all(copies, axis, split_axis=0, concat_axis=0, tiled=True)


def over_copies(x, axis):
    return sent_to_all(x, axis).sum(axis=0)


def in_order(parts, dim):
    parts = jnp.moveaxis(parts, 0, dim)
    lengths = parts.shape
    return parts.reshape(*lengths[:dim], lengths[dim] * lengths[dim + 1], *lengths[dim + 2 :])


def gathered_copies(x, axis, dim):
    return in_order(sent_to_all(x, axis), dim)


def over_copies_2(x, axis):
    return sent_to_all(x, axis).max(axis=0)


def over_axes(x, axes):
    far, near = axes
    nearer = over_copies_2(x, near)
    return over_copies_2(nearer, far)


def in_blocks(x, dim, count):
    before, after = (x.shape[:dim], x.shape[dim + 1 :])
    return jnp.moveaxis(x.reshape(*before, count, -1, *after), dim, 0)


def summed_on_arrival(x, axis, dim):
    count = lax.axis_size(axis)
    parts = lax.all_to_all(in_blocks(x, dim, count), axis, 0, 0, tiled=True)
    return jnp.sum(parts, axis=0)


def sum_in_two_steps(x, axes, dim):
    far, near = axes
    own = summed_on_arrival(in_blocks(x, dim, lax.axis_size(far)), near, dim + 1)
    return jnp.sum(lax.all_to_all(own, far, 0, 0, tiled=True), axis=0)


def side_by_side(arrays, axis, dim, along):
    columns = [a.reshape(*a.shape[:along], -1) for a in arrays]
    both = jnp.concatenate(columns, axis=along)
    filled, at, gathered = (sum_in_two_steps(both, axis, dim), 0, [])
    for a, column in zip(arrays, columns):
        share = filled[..., at : at + column.shape[along]]
        gathered.append(share.reshape(*share.shape[:along], *a.shape[along:]))
        at += column.shape[along]
    return tuple(gathered)


def turned_gather(arrays, axis, dims):
    turned = [jnp.moveaxis(a, dim, 0) for a, dim in zip(arrays, dims)]
    both = jnp.concatenate([t.reshape(len(t), -1) for t in turned], axis=1)
    filled, at, gathered = (lax.all_gather(both, axis, axis=0, tiled=True), 0, [])
    for t, dim in zip(turned, dims):
        share = filled[:, at : at + t[0].size].reshape(-1, *t.shape[1:])
        gathered.append(jnp.moveaxis(share, 0, dim))
        at += t[0].size
    return tuple(gathered)


def on_device(query_low, query_weight, latent_cache, lengths, value_weight, output_weight):
    ctx_count = lax.axis_size(CTX)
    head_count = lax.axis_size(HEAD)
    sequences = query_low.shape[0]
    local_heads = value_weight.shape[0]
    all_heads = local_heads * head_count
    per_share = local_heads // ctx_count
    width = latent_cache.shape[2]
    partial_value = jnp.dot(query_low, query_weight, preferred_element_type=jnp.float32)
    summed = over_copies(partial_value, CTX).astype(jnp.bfloat16)
    gathered = gathered_copies(summed, HEAD, 1)
    queries = gathered.reshape(sequences, all_heads, width)
    span = latent_cache.shape[1]
    offset = (lax.axis_index(CTX) * head_count + lax.axis_index(HEAD)) * span
    places = offset + jnp.arange(span, dtype=jnp.int32)
    usable = (places[None, :] < lengths[:, None])[:, None, :]
    scores = (
        jnp.einsum("bhc,bpc->bhp", queries, latent_cache, preferred_element_type=jnp.float32)
        * softmax_scale
    )
    scores = jnp.where(usable, scores, -1e30)
    local_max = jnp.max(scores, axis=2)
    probabilities = jnp.where(usable, jnp.exp(scores - local_max[..., None]), 0.0)
    totals = jnp.sum(probabilities, axis=2)
    numerators = jnp.einsum(
        "bhp,bpc->bhc",
        probabilities.astype(jnp.bfloat16),
        latent_cache[:, :, :KV_RANK],
        preferred_element_type=jnp.float32,
    )
    highest = over_axes(local_max, (("ctx_0", "ctx_1", "head_0"), "head_1"))
    factor = jnp.exp(local_max - highest)

    def regroup(values):
        dims_now = values.shape
        grouped = values.reshape((sequences, head_count, ctx_count, per_share) + dims_now[2:])
        return jnp.swapaxes(grouped, 1, 2).reshape(dims_now)

    share_totals, share_numerators = side_by_side(
        (regroup(totals * factor), regroup(numerators * factor[..., None])),
        (("ctx_0", "ctx_1", "head_0"), "head_1"),
        1,
        2,
    )
    head_totals, head_numerators = turned_gather((share_totals, share_numerators), CTX, (1, 1))
    latent_out = (head_numerators / head_totals[..., None]).astype(jnp.bfloat16)
    values = jnp.einsum(
        "bhc,hcv->bhv", latent_out, value_weight, preferred_element_type=jnp.float32
    ).astype(jnp.bfloat16)
    projected = jnp.dot(
        values.reshape(sequences, -1), output_weight, preferred_element_type=jnp.float32
    )
    return summed_on_arrival(projected, HEAD, 1).astype(jnp.bfloat16)


def solution(mesh):
    finer = Mesh(mesh.devices.reshape(4, 4, 4, 2), ("ctx_0", "ctx_1", "head_0", "head_1"))
    return jax.shard_map(
        on_device,
        mesh=finer,
        in_specs=(
            P(None, CTX),
            P(CTX, HEAD),
            P(None, CTX_HEAD, None),
            P(),
            P(HEAD, None, None),
            P(HEAD, CTX),
        ),
        out_specs=P(None, CTX_HEAD),
        check_vma=False,
    )
```

profile of v0, /device:TPU:1, one launch (start us, length us, event | category | flops | bytes accessed | tf_op | source)
XLA Modules:
  0.0 125.0 jit_solution(3201359506912485582)
XLA Ops:
  0.0 2.0 %fusion.23 = f32[2,9216]{1,0:T(2,128)S(1)} fusion(bf16[2,96]{1,0:T(2,128)(2,1)} %param.6, bf16[96,9216]{1,0:T(8,128)(2,1)} %param.7), kind=kOutput, calls=%fused_computation.30 | convolution fusion | flops 3538944 | bytes 1843584 | tf_op jit(solution)/shard_map/dot_general | solution.py:90
  2.0 1.3 %broadcast_in_dim.37 = f32[16,2,9216]{2,1,0:T(2,128)} broadcast(f32[2,9216]{1,0:T(2,128)S(1)} %fusion.23), dimensions={1,2} | broadcast | bytes 1253376 | tf_op jit(solution)/shard_map/broadcast_in_dim | solution.py:15
  3.3 7.7 %all-to-all-start = ((f32[16,2,9216]{2,1,0:T(2,128)}), f32[16,2,9216]{2,1,0:T(2,128)S(1)}, u32[]{:S(2)}, u32[]{:S(2)}) async-start(f32[16,2,9216]{2,1,0:T(2,128)} %broadcast_in_dim.37), calls=%async_computation | async-start | bytes 2359296 | tf_op jit(solution)/shard_map/all_to_all | solution.py:16
  11.0 17.0 %all-to-all-done = f32[16,2,9216]{2,1,0:T(2,128)S(1)} async-done(((f32[16,2,9216]{2,1,0:T(2,128)}), f32[16,2,9216]{2,1,0:T(2,128)S(1)}, u32[]{:S(2)}, u32[]{:S(2)}) %all-to-all-start) | async-done | bytes 1179680 | tf_op jit(solution)/shard_map/all_to_all | solution.py:16
  28.0 0.4 reduce_sum.49
  28.4 0.9 broadcast_in_dim.38
  29.3 8.6 %all-to-all-start.1 = ((bf16[8,2,9216]{2,1,0:T(2,128)(2,1)}), bf16[8,2,9216]{2,1,0:T(2,128)(2,1)S(1)}, u32[]{:S(2)}, u32[]{:S(2)}) async-start(bf16[8,2,9216]{2,1,0:T(2,128)(2,1)} %broadcast_in_dim.38), calls=%async_computation.1 | async-start | bytes 589824 | tf_op jit(solution)/shard_map/all_to_all | solution.py:16
  37.9 6.7 %all-to-all-done.1 = bf16[8,2,9216]{2,1,0:T(2,128)(2,1)S(1)} async-done(((bf16[8,2,9216]{2,1,0:T(2,128)(2,1)}), bf16[8,2,9216]{2,1,0:T(2,128)(2,1)S(1)}, u32[]{:S(2)}, u32[]{:S(2)}) %all-to-all-start.1) | async-done | bytes 294944 | tf_op jit(solution)/shard_map/all_to_all | solution.py:16
  45.0 2.4 %fusion.22 = (f32[2,128]{1,0:T(2,128)S(1)}, f32[2,128,1024]{2,1,0:T(8,128)S(1)}) fusion(bf16[2,128,576]{2,1,0:T(8,128)(2,1)S(1)} %reshape_reshape.4, bf16[2,1024,576]{1,2,0:T(8,128)(2,1)} %param.8, pred[2,1024]{1,0:T(4,128)(4,1)S(1)} %broadcast_compare_fusion), kind=kOutput, calls=%fused_computation.29 | convolution fusion | flops 302776064 | bytes 3705856 | tf_op jit(solution)/shard_map/bhc,bpc->bhp/dot_general | solution.py:99
  47.4 4.4 %all_to_all.35 = f32[2,2,128]{2,1,0:T(2,128)S(1)} all-to-all(f32[2,2,128]{2,1,0:T(2,128)S(1)} %broadcast_in_dim.41), channel_id=1, replica_groups=mesh['ctx_0'=4,'ctx_1'=4,'head_0'=4,'head_1'=2] {'head_1'}, dimensions={0} | all-to-all | bytes 4096 | tf_op jit(solution)/shard_map/all_to_all | solution.py:16
  51.8 0.6 broadcast_in_dim.42
  52.5 4.6 %all-to-all-start.3 = ((f32[64,2,128]{2,1,0:T(2,128)}), f32[64,2,128]{2,1,0:T(2,128)S(1)}, u32[]{:S(2)}, u32[]{:S(2)}) async-start(f32[64,2,128]{2,1,0:T(2,128)} %broadcast_in_dim.42), calls=%async_computation.3 | async-start | bytes 131072 | tf_op jit(solution)/shard_map/all_to_all | solution.py:16
  57.1 0.3 fusion.10
  57.4 8.1 %all-to-all-done.3 = f32[64,2,128]{2,1,0:T(2,128)S(1)} async-done(((f32[64,2,128]{2,1,0:T(2,128)}), f32[64,2,128]{2,1,0:T(2,128)S(1)}, u32[]{:S(2)}, u32[]{:S(2)}) %all-to-all-start.3) | async-done | bytes 65568 | tf_op jit(solution)/shard_map/all_to_all | solution.py:16
  65.6 2.4 %fusion.3 = f32[2,128,512]{2,1,0:T(8,128)S(1)} fusion(bf16[2,1024,576]{1,2,0:T(8,128)(2,1)} %param.8, f32[2,128,1024]{2,1,0:T(8,128)S(1)} %get-tuple-element.8, f32[2,128]{1,0:T(2,128)S(1)} %get-tuple-element.7, pred[2,1024]{1,0:T(4,128)(4,1)S(1)} %broadcast_compare_fusion, f32[2,128]{1,0:T(2,128)S(1)} %get-tuple-element.6), kind=kOutput, calls=%fused_computation.4 | convolution fusion | flops 269352960 | bytes 3674112 | tf_op jit(solution)/shard_map/bhp,bpc->bhc/dot_general | solution.py:106
  68.1 0.4 copy.37
  68.8 0.7 maximum_bitcast_fusion
  69.7 5.6 %all_to_all.36 = f32[2,64,2,1,513]{4,2,1,3,0:T(2,128)S(1)} all-to-all(f32[2,64,2,1,513]{4,2,1,3,0:T(2,128)S(1)} %copy.39), channel_id=1, replica_groups=mesh['ctx_0'=4,'ctx_1'=4,'head_0'=4,'head_1'=2] {'head_1'}, dimensions={0} | all-to-all | bytes 1050624 | tf_op jit(solution)/shard_map/all_to_all | solution.py:50
  75.3 0.6 reduce_sum.51
  75.9 14.7 %all_to_all.37 = f32[64,2,1,513]{3,1,2,0:T(2,128)S(1)} all-to-all(f32[64,2,1,513]{3,1,2,0:T(2,128)S(1)} %bitcast.59), channel_id=1, replica_groups=mesh['ctx_0'=4,'ctx_1'=4,'head_0'=4,'head_1'=2] {'ctx_0','ctx_1','head_0'}, dimensions={0} | all-to-all | bytes 525312 | tf_op jit(solution)/shard_map/all_to_all | solution.py:57
  91.0 16.2 %all-gather = f32[16,1,1026]{2,1,0:T(1,128)S(1)} all-gather(f32[1,1,1026]{2,1,0:T(1,128)S(1)} %maximum_bitcast_fusion.1), channel_id=1, replica_groups=mesh['ctx_0'=4,'ctx_1'=4,'head_0'=4,'head_1'=2] {'ctx_0','ctx_1'}, dimensions={0}, use_global_device_ids=true | all-gather | bytes 69768 | tf_op jit(solution)/shard_map/all_gather | solution.py:74
  107.4 2.7 %fusion.8 = f32[8,2,56]{2,1,0:T(2,128)S(1)} fusion(bf16[8,56,2048]{2,1,0:T(8,128)(2,1)} %bitcast.58, bf16[16,512,128]{2,1,0:T(8,128)(2,1)S(1)} %copy-done, f32[16,2,512]{2,1,0:T(2,128)S(1)} %reshape.93, f32[2,16]{0,1:T(8,128)S(1)} %slice_bitcast_fusion), kind=kOutput, calls=%fused_computation.8 | convolution fusion | flops 7901184 | bytes 4001408 | tf_op jit(solution)/shard_map/dot_general | solution.py:131
  110.1 14.3 %all_to_all.38 = f32[8,2,56]{2,1,0:T(2,128)S(1)} all-to-all(f32[8,2,56]{2,1,0:T(2,128)S(1)} %fusion.8), channel_id=1, replica_groups=mesh['ctx_0'=4,'ctx_1'=4,'head_0'=4,'head_1'=2] {'head_0','head_1'}, dimensions={0} | all-to-all | bytes 7168 | tf_op jit(solution)/shard_map/all_to_all | solution.py:50
  124.5 0.5 reduce_sum.55
  (25 shorter events, 1.5 us)
Async XLA Ops:
  0.0 107.4 %copy-start = (bf16[16,512,128]{2,1,0:T(8,128)(2,1)S(1)}, bf16[16,512,128]{2,1,0:T(8,128)(2,1)}, u32[]{:S(2)}) copy-start(bf16[16,512,128]{2,1,0:T(8,128)(2,1)} %param.10) | copy-start | bytes 6291460
  3.3 34.6 %copy-start.1 = (s32[2]{0:T(128)S(1)}, s32[2]{0:T(128)}, u32[]{:S(2)}) copy-start(s32[2]{0:T(128)} %param.9) | copy-start | bytes 28
  3.3 24.7 %all-to-all-start = ((f32[16,2,9216]{2,1,0:T(2,128)}), f32[16,2,9216]{2,1,0:T(2,128)S(1)}, u32[]{:S(2)}, u32[]{:S(2)}) async-start(f32[16,2,9216]{2,1,0:T(2,128)} %broadcast_in_dim.37), calls=%async_computation | async-start | bytes 2359296 | tf_op jit(solution)/shard_map/all_to_all | solution.py:16
  29.3 15.3 %all-to-all-start.1 = ((bf16[8,2,9216]{2,1,0:T(2,128)(2,1)}), bf16[8,2,9216]{2,1,0:T(2,128)(2,1)S(1)}, u32[]{:S(2)}, u32[]{:S(2)}) async-start(bf16[8,2,9216]{2,1,0:T(2,128)(2,1)} %broadcast_in_dim.38), calls=%async_computation.1 | async-start | bytes 589824 | tf_op jit(solution)/shard_map/all_to_all | solution.py:16
  52.5 13.1 %all-to-all-start.3 = ((f32[64,2,128]{2,1,0:T(2,128)}), f32[64,2,128]{2,1,0:T(2,128)S(1)}, u32[]{:S(2)}, u32[]{:S(2)}) async-start(f32[64,2,128]{2,1,0:T(2,128)} %broadcast_in_dim.42), calls=%async_computation.3 | async-start | bytes 131072 | tf_op jit(solution)/shard_map/all_to_all | solution.py:16
where the time goes:
time: 126 us; the launch traced here: 125 us
  blocking collectives  55.4 us (44%)
  waiting for transfers between devices  31.8 us (25%)
  starting transfers between devices  20.9 us (17%)
  matrix products  9.5 us (8%)
  local copies, waits for them, and re-layouts  4.34 us (3%)
  other arithmetic  2.99 us (2%)
    all_to_all x3, waiting for transfers between devices, sent_to_all(): return lax.all_to_all(copies, axis, split_axis=0, concat_axis=0, tiled=True)  31.8 us
    all_to_all x3, starting transfers between devices, sent_to_all(): return lax.all_to_all(copies, axis, split_axis=0, concat_axis=0, tiled=True)  20.9 us
    all_to_all x2, blocking collectives, summed_on_arrival(): parts = lax.all_to_all(in_blocks(x, dim, count), axis, 0, 0, tiled=True)  20 us
    all_gather x1, blocking collectives, turned_gather(): lax.all_gather(both, axis, axis=0, tiled=True)  16.2 us
    all_to_all x1, blocking collectives, sum_in_two_steps(): return jnp.sum(lax.all_to_all(own, far, 0, 0, tiled=True), axis=0)  14.7 us
    all_to_all x1, blocking collectives, sent_to_all(): return lax.all_to_all(copies, axis, split_axis=0, concat_axis=0, tiled=True)  4.44 us
    broadcast_in_dim x4, local copies, waits for them, and re-layouts, sent_to_all(): copies = jnp.broadcast_to(x, (lax.axis_size(axis), *x.shape))  2.82 us
    dot_general x1, matrix products, on_device(): jnp.dot(values.reshape(sequences, -1), output_weight, preferred_element_t...  2.71 us
  transfers between devices with their start and end apart: 3, of which 3 were waited for; matrix products, arithmetic and copies ran while one was open for 0% of the time, Pallas kernels for 0%

commit v1 on v0

--- a/solution.py
+++ b/solution.py
@@ -71,7 +71,19 @@
 def turned_gather(arrays, axis, dims):
     turned = [jnp.moveaxis(a, dim, 0) for a, dim in zip(arrays, dims)]
     both = jnp.concatenate([t.reshape(len(t), -1) for t in turned], axis=1)
-    filled, at, gathered = (lax.all_gather(both, axis, axis=0, tiled=True), 0, [])
+    filled, at, gathered = (
+        jnp.concatenate(
+            lax.all_to_all(
+                jnp.stack([both for _ in range(lax.axis_size(axis))], axis=0),
+                axis,
+                split_axis=0,
+                concat_axis=0,
+            ),
+            axis=0,
+        ),
+        0,
+        [],
+    )
     for t, dim in zip(turned, dims):
         share = filled[:, at : at + t[0].size].reshape(-1, *t.shape[1:])
         gathered.append(jnp.moveaxis(share, 0, dim))

time: 126 us -> 115 us (0.913)
  blocking collectives: 55.4 us -> 44.4 us
    all_gather x1 -> x0, blocking collectives: 16.2 us -> none  [turned_gather(): lax.all_gather(both, axis, axis=0, tiled=True)]
    all_to_all x0 -> x1, blocking collectives: none -> 9.29 us  [turned_gather(): lax.all_to_all(jnp.stack([both for _ in range(lax.axis_size(axis))], axis...]
    all_to_all x2, blocking collectives: 20 us -> 15.9 us  [summed_on_arrival(): parts = lax.all_to_all(in_blocks(x, dim, count), axis, 0, 0, tiled=True)]
where the time goes in v1:
time: 115 us; the launch traced here: 114 us
  blocking collectives  44.4 us (39%)
  waiting for transfers between devices  31.8 us (28%)
  starting transfers between devices  20.9 us (18%)
  matrix products  9.5 us (8%)
  local copies, waits for them, and re-layouts  4.38 us (4%)
  other arithmetic  3 us (3%)
    all_to_all x3, waiting for transfers between devices, sent_to_all(): return lax.all_to_all(copies, axis, split_axis=0, concat_axis=0, tiled=True)  31.8 us
    all_to_all x3, starting transfers between devices, sent_to_all(): return lax.all_to_all(copies, axis, split_axis=0, concat_axis=0, tiled=True)  20.9 us
    all_to_all x2, blocking collectives, summed_on_arrival(): parts = lax.all_to_all(in_blocks(x, dim, count), axis, 0, 0, tiled=True)  15.9 us
    all_to_all x1, blocking collectives, sum_in_two_steps(): return jnp.sum(lax.all_to_all(own, far, 0, 0, tiled=True), axis=0)  14.7 us
    all_to_all x1, blocking collectives, turned_gather(): lax.all_to_all(jnp.stack([both for _ in range(lax.axis_size(axis))], axis...  9.29 us
    all_to_all x1, blocking collectives, sent_to_all(): return lax.all_to_all(copies, axis, split_axis=0, concat_axis=0, tiled=True)  4.44 us
    broadcast_in_dim x4, local copies, waits for them, and re-layouts, sent_to_all(): copies = jnp.broadcast_to(x, (lax.axis_size(axis), *x.shape))  2.82 us
    dot_general x1, matrix products, on_device(): jnp.dot(values.reshape(sequences, -1), output_weight, preferred_element_t...  2.71 us
  transfers between devices with their start and end apart: 3, of which 3 were waited for; matrix products, arithmetic and copies ran while one was open for 0% of the time, Pallas kernels for 0%

profile of v1, /device:TPU:1, one launch (start us, length us, event | category | flops | bytes accessed | tf_op | source)
XLA Modules:
  0.0 114.1 jit_solution(16575330218785610403)
XLA Ops:
  0.0 2.0 %fusion.23 = f32[2,9216]{1,0:T(2,128)S(1)} fusion(bf16[2,96]{1,0:T(2,128)(2,1)} %param.6, bf16[96,9216]{1,0:T(8,128)(2,1)} %param.7), kind=kOutput, calls=%fused_computation.30 | convolution fusion | flops 3538944 | bytes 1843584 | tf_op jit(solution)/shard_map/dot_general | solution.py:102
  2.0 1.3 %broadcast_in_dim.37 = f32[16,2,9216]{2,1,0:T(2,128)} broadcast(f32[2,9216]{1,0:T(2,128)S(1)} %fusion.23), dimensions={1,2} | broadcast | bytes 1253376 | tf_op jit(solution)/shard_map/broadcast_in_dim | solution.py:15
  3.3 7.7 %all-to-all-start = ((f32[16,2,9216]{2,1,0:T(2,128)}), f32[16,2,9216]{2,1,0:T(2,128)S(1)}, u32[]{:S(2)}, u32[]{:S(2)}) async-start(f32[16,2,9216]{2,1,0:T(2,128)} %broadcast_in_dim.37), calls=%async_computation | async-start | bytes 2359296 | tf_op jit(solution)/shard_map/all_to_all | solution.py:16
  11.0 17.0 %all-to-all-done = f32[16,2,9216]{2,1,0:T(2,128)S(1)} async-done(((f32[16,2,9216]{2,1,0:T(2,128)}), f32[16,2,9216]{2,1,0:T(2,128)S(1)}, u32[]{:S(2)}, u32[]{:S(2)}) %all-to-all-start) | async-done | bytes 1179680 | tf_op jit(solution)/shard_map/all_to_all | solution.py:16
  28.0 0.4 reduce_sum.49
  28.4 0.9 broadcast_in_dim.38
  29.3 8.6 %all-to-all-start.1 = ((bf16[8,2,9216]{2,1,0:T(2,128)(2,1)}), bf16[8,2,9216]{2,1,0:T(2,128)(2,1)S(1)}, u32[]{:S(2)}, u32[]{:S(2)}) async-start(bf16[8,2,9216]{2,1,0:T(2,128)(2,1)} %broadcast_in_dim.38), calls=%async_computation.1 | async-start | bytes 589824 | tf_op jit(solution)/shard_map/all_to_all | solution.py:16
  37.9 6.7 %all-to-all-done.1 = bf16[8,2,9216]{2,1,0:T(2,128)(2,1)S(1)} async-done(((bf16[8,2,9216]{2,1,0:T(2,128)(2,1)}), bf16[8,2,9216]{2,1,0:T(2,128)(2,1)S(1)}, u32[]{:S(2)}, u32[]{:S(2)}) %all-to-all-start.1) | async-done | bytes 294944 | tf_op jit(solution)/shard_map/all_to_all | solution.py:16
  45.0 2.4 %fusion.22 = (f32[2,128]{1,0:T(2,128)S(1)}, f32[2,128,1024]{2,1,0:T(8,128)S(1)}) fusion(bf16[2,128,576]{2,1,0:T(8,128)(2,1)S(1)} %reshape_reshape.4, bf16[2,1024,576]{1,2,0:T(8,128)(2,1)} %param.8, pred[2,1024]{1,0:T(4,128)(4,1)S(1)} %broadcast_compare_fusion), kind=kOutput, calls=%fused_computation.29 | convolution fusion | flops 302776064 | bytes 3705856 | tf_op jit(solution)/shard_map/bhc,bpc->bhp/dot_general | solution.py:111
  47.4 4.4 %all_to_all.40 = f32[2,2,128]{2,1,0:T(2,128)S(1)} all-to-all(f32[2,2,128]{2,1,0:T(2,128)S(1)} %broadcast_in_dim.41), channel_id=1, replica_groups=mesh['ctx_0'=4,'ctx_1'=4,'head_0'=4,'head_1'=2] {'head_1'}, dimensions={0} | all-to-all | bytes 4096 | tf_op jit(solution)/shard_map/all_to_all | solution.py:16
  51.8 0.6 broadcast_in_dim.42
  52.5 4.6 %all-to-all-start.3 = ((f32[64,2,128]{2,1,0:T(2,128)}), f32[64,2,128]{2,1,0:T(2,128)S(1)}, u32[]{:S(2)}, u32[]{:S(2)}) async-start(f32[64,2,128]{2,1,0:T(2,128)} %broadcast_in_dim.42), calls=%async_computation.3 | async-start | bytes 131072 | tf_op jit(solution)/shard_map/all_to_all | solution.py:16
  57.1 0.3 fusion.10
  57.4 8.1 %all-to-all-done.3 = f32[64,2,128]{2,1,0:T(2,128)S(1)} async-done(((f32[64,2,128]{2,1,0:T(2,128)}), f32[64,2,128]{2,1,0:T(2,128)S(1)}, u32[]{:S(2)}, u32[]{:S(2)}) %all-to-all-start.3) | async-done | bytes 65568 | tf_op jit(solution)/shard_map/all_to_all | solution.py:16
  65.6 2.4 %fusion.3 = f32[2,128,512]{2,1,0:T(8,128)S(1)} fusion(bf16[2,1024,576]{1,2,0:T(8,128)(2,1)} %param.8, f32[2,128,1024]{2,1,0:T(8,128)S(1)} %get-tuple-element.8, f32[2,128]{1,0:T(2,128)S(1)} %get-tuple-element.7, pred[2,1024]{1,0:T(4,128)(4,1)S(1)} %broadcast_compare_fusion, f32[2,128]{1,0:T(2,128)S(1)} %get-tuple-element.6), kind=kOutput, calls=%fused_computation.4 | convolution fusion | flops 269352960 | bytes 3674112 | tf_op jit(solution)/shard_map/bhp,bpc->bhc/dot_general | solution.py:118
  68.1 0.4 copy.37
  68.8 0.7 maximum_bitcast_fusion
  69.7 5.6 %all_to_all.41 = f32[2,64,2,1,513]{4,2,1,3,0:T(2,128)S(1)} all-to-all(f32[2,64,2,1,513]{4,2,1,3,0:T(2,128)S(1)} %copy.39), channel_id=1, replica_groups=mesh['ctx_0'=4,'ctx_1'=4,'head_0'=4,'head_1'=2] {'head_1'}, dimensions={0} | all-to-all | bytes 1050624 | tf_op jit(solution)/shard_map/all_to_all | solution.py:50
  75.3 0.6 reduce_sum.51
  75.9 14.7 %all_to_all.42 = f32[64,2,1,513]{3,1,2,0:T(2,128)S(1)} all-to-all(f32[64,2,1,513]{3,1,2,0:T(2,128)S(1)} %bitcast.57), channel_id=1, replica_groups=mesh['ctx_0'=4,'ctx_1'=4,'head_0'=4,'head_1'=2] {'ctx_0','ctx_1','head_0'}, dimensions={0} | all-to-all | bytes 525312 | tf_op jit(solution)/shard_map/all_to_all | solution.py:57
  91.1 9.3 %all_to_all.43 = f32[16,1,1026]{2,1,0:T(1,128)S(1)} all-to-all(f32[16,1,1026]{2,1,0:T(1,128)S(1)} %stack.2), channel_id=1, replica_groups=mesh['ctx_0'=4,'ctx_1'=4,'head_0'=4,'head_1'=2] {'ctx_0','ctx_1'}, dimensions={0} | all-to-all | bytes 131328 | tf_op jit(solution)/shard_map/all_to_all | solution.py:76
  100.6 2.7 %fusion.8 = f32[8,2,56]{2,1,0:T(2,128)S(1)} fusion(bf16[8,56,2048]{2,1,0:T(8,128)(2,1)} %bitcast.56, bf16[16,512,128]{2,1,0:T(8,128)(2,1)S(1)} %copy-done, f32[16,2,512]{2,1,0:T(2,128)S(1)} %reshape.100, f32[2,16]{0,1:T(8,128)S(1)} %slice_bitcast_fusion), kind=kOutput, calls=%fused_computation.8 | convolution fusion | flops 7901184 | bytes 4001408 | tf_op jit(solution)/shard_map/dot_general | solution.py:143
  103.3 10.3 %all_to_all.44 = f32[8,2,56]{2,1,0:T(2,128)S(1)} all-to-all(f32[8,2,56]{2,1,0:T(2,128)S(1)} %fusion.8), channel_id=1, replica_groups=mesh['ctx_0'=4,'ctx_1'=4,'head_0'=4,'head_1'=2] {'head_0','head_1'}, dimensions={0} | all-to-all | bytes 7168 | tf_op jit(solution)/shard_map/all_to_all | solution.py:50
  113.6 0.5 reduce_sum.55
  (26 shorter events, 1.6 us)
Async XLA Ops:
  0.0 100.6 %copy-start = (bf16[16,512,128]{2,1,0:T(8,128)(2,1)S(1)}, bf16[16,512,128]{2,1,0:T(8,128)(2,1)}, u32[]{:S(2)}) copy-start(bf16[16,512,128]{2,1,0:T(8,128)(2,1)} %param.10) | copy-start | bytes 6291460
  3.3 34.6 %copy-start.1 = (s32[2]{0:T(128)S(1)}, s32[2]{0:T(128)}, u32[]{:S(2)}) copy-start(s32[2]{0:T(128)} %param.9) | copy-start | bytes 28
  3.3 24.7 %all-to-all-start = ((f32[16,2,9216]{2,1,0:T(2,128)}), f32[16,2,9216]{2,1,0:T(2,128)S(1)}, u32[]{:S(2)}, u32[]{:S(2)}) async-start(f32[16,2,9216]{2,1,0:T(2,128)} %broadcast_in_dim.37), calls=%async_computation | async-start | bytes 2359296 | tf_op jit(solution)/shard_map/all_to_all | solution.py:16
  29.3 15.3 %all-to-all-start.1 = ((bf16[8,2,9216]{2,1,0:T(2,128)(2,1)}), bf16[8,2,9216]{2,1,0:T(2,128)(2,1)S(1)}, u32[]{:S(2)}, u32[]{:S(2)}) async-start(bf16[8,2,9216]{2,1,0:T(2,128)(2,1)} %broadcast_in_dim.38), calls=%async_computation.1 | async-start | bytes 589824 | tf_op jit(solution)/shard_map/all_to_all | solution.py:16
  52.5 13.1 %all-to-all-start.3 = ((f32[64,2,128]{2,1,0:T(2,128)}), f32[64,2,128]{2,1,0:T(2,128)S(1)}, u32[]{:S(2)}, u32[]{:S(2)}) async-start(f32[64,2,128]{2,1,0:T(2,128)} %broadcast_in_dim.42), calls=%async_computation.3 | async-start | bytes 131072 | tf_op jit(solution)/shard_map/all_to_all | solution.py:16
